TPU v7x, 32 devices: a whole 2x2x4 slice. The times are simulated.
32 devices in a mesh: pw: 2 (over x), pair: 16 (over z, y, core).
Axes of the slice: x: 2, y: 2, z: 4, core: 2. Of those that a mesh axis runs over, the one named last changes fastest.
Arguments:
- valence_pairs: bfloat16 [64, 64, 8192], P('pair', None, 'pw'), may hold values from -0.59765625 to 0.59765625
- conduction_pairs: bfloat16 [16, 256, 8192], P('pair', None, 'pw'), may hold values from -0.59765625 to 0.59765625
- screening: float32 [8192], P('pw'), may hold values from 0.1 to 2
Outputs:
- kernel: float32 [64, 16, 64, 256], P('pair', None, 'pw')
All inputs are finite; a program needn't handle non-finite values.
Results may differ from a plain program's by a relative error of at most 0.0029.
Values may be sent and summed in bfloat16 or wider, within the bound.
A program may use at most 128 MiB of HBM per device.

v0:
```python
import jax
import jax.numpy as jnp
from jax import lax
from jax.sharding import PartitionSpec as P


def contract(piece, flat_right, band_dev, conduction):
    first, second, width = piece.shape
    product = lax.dot_general(
        piece.reshape(first * second, width),
        flat_right,
        (((1,), (1,)), ((), ())),
        preferred_element_type=jnp.float32,
    )
    return product.reshape(first, second, band_dev, conduction)


def route_rows(terms):
    owned = lax.all_to_all(terms, "pair", split_axis=0, concat_axis=2, tiled=True)
    return owned.transpose(0, 2, 1, 3)


def body(valence_pairs, conduction_pairs, screening):
    screened = (valence_pairs.astype(jnp.float32) * screening[None, None, :]).astype(jnp.bfloat16)
    band_dev, conduction, plane_dev = conduction_pairs.shape
    flat_local = conduction_pairs.reshape(band_dev * conduction, plane_dev)
    partial_value = contract(
        lax.all_gather(screened, "pair", axis=0, tiled=True), flat_local, band_dev, conduction
    )
    terms = lax.psum_scatter(partial_value, "pw", scatter_dimension=1, tiled=True)
    return route_rows(terms)


def solution(mesh):
    placed = (P("pair", None, "pw"), P("pair", None, "pw"), P("pw"))
    return jax.shard_map(
        body, mesh=mesh, in_specs=placed, out_specs=P("pair", None, "pw", None), check_vma=False
    )
```

profile of v0, /device:TPU:12, one launch (start us, length us, event | category | flops | bytes accessed | tf_op | source)
XLA Modules:
  0.0 312.5 jit_solution(8804609150901646009)
XLA Ops:
  6.5 0.0 copy-start
  6.5 0.0 all-gather.2.cloned.1.call-start
  6.5 3.5 %multiply_convert_fusion = bf16[4,64,4096]{2,1,0:T(8,128)(2,1)} fusion(bf16[4,64,4096]{2,1,0:T(8,128)(2,1)} %param.3, f32[4096]{0:T(1024)} %param.5), kind=kLoop, calls=%fused_computation | loop fusion | flops 3145728 | bytes 4210688 | tf_op jit(solution)/shard_map/convert_element_type | solution.py:24
  10.1 0.0 all-gather.2.cloned.1.call-update
  10.1 0.0 reduce-scatter.2.cloned.1.call-start
  10.1 168.9 %all-gather.2.cloned.1.call-done = bf16[64,64,4096]{2,1,0:T(8,128)(2,1)} async-done(((bf16[4,64,4096]{2,1,0:T(8,128)(2,1)}), bf16[64,64,4096]{2,1,0:T(8,128)(2,1)}) %all-gather.2.cloned.1.call-update) | async-done | bytes 33554448 | tf_op jit(solution)/shard_map/all_gather | solution.py:28
  179.0 0.0 copy-done
  179.0 17.2 %convolution_bitcast_fusion = f32[64,64,1,256]{3,1,0,2:T(8,128)} fusion(bf16[64,64,4096]{2,1,0:T(8,128)(2,1)} %all-gather.2.cloned.1.call-done, bf16[1,256,4096]{2,1,0:T(8,128)(2,1)S(1)} %copy-done), kind=kOutput, calls=%fused_computation.1 | convolution fusion | flops 8589934592 | bytes 39845888 | tf_op jit(solution)/shard_map/dot_general | solution.py:9
  196.2 0.0 reduce-scatter.2.cloned.1.call-update
  196.2 54.9 %reduce-scatter.2.cloned.1.call-done = f32[64,32,1,256]{3,1,0,2:T(8,128)} async-done(((f32[64,64,1,256]{3,1,0,2:T(8,128)}), f32[64,32,1,256]{3,1,0,2:T(8,128)}) %reduce-scatter.2.cloned.1.call-update) | async-done | bytes 2097168 | tf_op jit(solution)/shard_map/reduce_scatter | solution.py:30
  251.1 53.1 %all_to_all.18 = f32[64,32,1,256]{3,1,2,0:T(8,128)S(1)} all-to-all(f32[64,32,1,256]{3,1,2,0:T(8,128)} %bitcast.17), channel_id=1, replica_groups=mesh['pw'=2,'pair'=16] {'pair'}, dimensions={0} | all-to-all | bytes 4194304 | tf_op jit(solution)/shard_map/all_to_all | solution.py:19
  304.2 1.5 copy.8
Async XLA Ops:
  6.5 172.5 %copy-start = (bf16[1,256,4096]{2,1,0:T(8,128)(2,1)S(1)}, bf16[1,256,4096]{2,1,0:T(8,128)(2,1)}, u32[]{:S(2)}) copy-start(bf16[1,256,4096]{2,1,0:T(8,128)(2,1)} %param.4) | copy-start | bytes 6291460
  6.5 172.5 %all-gather.2.cloned.1.call-start = ((), (), s32[]{:S(2)}) async-start(), calls=%async_computation.2 | async-start | bytes 35651584 | tf_op jit(solution)/shard_map/all_gather | solution.py:28
  10.1 241.0 %reduce-scatter.2.cloned.1.call-start = ((), (), s32[]{:S(2)}) async-start(), calls=%async_computation.3 | async-start | bytes 6291456 | tf_op jit(solution)/shard_map/reduce_scatter | solution.py:30
Sparse Core Ops, SparseCore 0:
  10.2 168.7 all-gather.1
  196.4 54.7 reduce-scatter.1
where the time goes:
time: 314 us; the launch traced here: 312 us
  waiting for transfers between devices  224 us (71%)
  blocking collectives  53.1 us (17%)
  matrix products  17.2 us (5%)
  between operations  13.4 us (4%)
  other arithmetic  3.53 us (1%)
    all_gather x1, waiting for transfers between devices, body(): lax.all_gather(screened, 'pair', axis=0, tiled=True)  169 us
    reduce_scatter x1, waiting for transfers between devices, body(): lax.psum_scatter(partial_value, 'pw', scatter_dimension=1, tiled=True)  54.9 us
    all_to_all x1, blocking collectives, route_rows(): lax.all_to_all(terms, 'pair', split_axis=0, concat_axis=2, tiled=True)  53.1 us
    dot_general x1, matrix products, contract(): lax.dot_general(piece.reshape(first * second, width), flat_right, (((1,),...  17.2 us
  transfers between devices with their start and end apart: 2, of which 2 were waited for; matrix products, arithmetic and copies ran while one was open for 0% of the time, Pallas kernels for 0%

commit v1 on v0

v1 whole, which is shorter than its diff:
```python
import functools

import jax
import jax.numpy as jnp
from jax import lax
from jax.experimental import pallas as pl
from jax.experimental.pallas import tpu as pltpu
from jax.sharding import PartitionSpec as P

MESH = pl.DeviceIdType.MESH
SIDE = 4
CHUNKS = 4


def contract(piece, flat_right, band_dev, conduction):
    first, second, width = piece.shape
    product = lax.dot_general(
        piece.reshape(first * second, width),
        flat_right,
        (((1,), (1,)), ((), ())),
        preferred_element_type=jnp.float32,
    )
    return product.reshape(first, second, band_dev, conduction)


def general_body(valence_pairs, conduction_pairs, screening):
    screened = (valence_pairs.astype(jnp.float32) * screening[None, None, :]).astype(jnp.bfloat16)
    band_dev, conduction, plane_dev = conduction_pairs.shape
    flat_local = conduction_pairs.reshape(band_dev * conduction, plane_dev)
    partial_value = contract(
        lax.all_gather(screened, "pair", axis=0, tiled=True), flat_local, band_dev, conduction
    )
    terms = lax.psum_scatter(partial_value, "pw", scatter_dimension=1, tiled=True)
    owned = lax.all_to_all(terms, "pair", split_axis=0, concat_axis=2, tiled=True)
    return owned.transpose(0, 2, 1, 3)


def flip(bit, by):
    return bit + by - 2 * bit * by


def grid_kernel(
    val, con, scr_row, out, raw, scr, bb, acc, xs, xr, zs, zr,
    loc, a1s, a1r, a2s, a2r, a3s, a3r, b1s, b1r, b2s, b2r, b3s, b3r, xss, xsr, zss, zsr,
):
    me, x = lax.axis_index("pair"), lax.axis_index("pw")
    core, y, zl, zh = me % 2, (me // 2) % 2, (me // 4) % 2, me // 8
    rows, depth = val.shape
    cols = con.shape[0]
    half = out.shape[2]
    step = rows // CHUNKS
    cstep = cols // CHUNKS

    def at(fc, fy, fl, fh):
        return (x, flip(core, fc) + 2 * flip(y, fy) + 4 * flip(zl, fl) + 8 * flip(zh, fh))

    def remote(src, dst, s, r, dev):
        return pltpu.make_async_remote_copy(
            src_ref=src, dst_ref=dst, send_sem=s, recv_sem=r, device_id=dev, device_id_type=MESH
        )

    def arows(k):
        return pl.ds(pl.multiple_of(k * step, step), step)

    def brows(k):
        return pl.ds(pl.multiple_of(k * cstep, cstep), cstep)

    sibling, beside, near, far = at(1, 0, 0, 0), at(0, 1, 0, 0), at(0, 0, 1, 0), at(0, 0, 0, 1)
    a1 = remote(val, raw.at[1], a1s.at[0], a1r.at[0], sibling)
    b1 = remote(con, bb.at[1], b1s.at[0], b1r.at[0], beside)

    def a2(k):
        return remote(val.at[arows(k)], raw.at[2, arows(k)], a2s.at[k], a2r.at[k], near)

    def b2(k):
        return remote(con.at[brows(k)], bb.at[2, brows(k)], b2s.at[k], b2r.at[k], far)

    def a3(k):
        return remote(raw.at[2, arows(k)], raw.at[3, arows(k)], a3s.at[k], a3r.at[k], sibling)

    def b3(k):
        return remote(bb.at[2, brows(k)], bb.at[3, brows(k)], b3s.at[k], b3r.at[k], beside)

    def xcopy(t):
        return remote(xs.at[t], xr.at[t], xss.at[t], xsr.at[t], (1 - x, me))

    def zcopy(t):
        a = t // SIDE
        return remote(zs.at[t], zr.at[t], zss.at[t], zsr.at[t], at(a % 2, 0, a // 2, 0))

    def each(n, fn, lo=0):
        def run(k, carry):
            fn(k)
            return carry
        lax.fori_loop(lo, n, run, 0)

    barrier = pltpu.get_barrier_semaphore()
    greeted = (sibling, beside, near, far, at(1, 0, 1, 0), (1 - x, me))
    for dev in greeted:
        pl.semaphore_signal(barrier, inc=1, device_id=dev, device_id_type=MESH)
    own_a = pltpu.make_async_copy(val, raw.at[0], loc.at[0])
    own_b = pltpu.make_async_copy(con, bb.at[0], loc.at[1])
    own_a.start()
    own_b.start()
    pl.semaphore_wait(barrier, len(greeted))

    end = zl == zh

    @pl.when(end)
    def _():
        each(CHUNKS, lambda k: a2(k).start())
        each(CHUNKS, lambda k: b2(k).start())

    @pl.when(jnp.logical_not(end))
    def _():
        each(CHUNKS, lambda k: b2(k).start())

    b1.start()
    a1.start()

    def screen(a):
        def part(i):
            r = pl.ds(pl.multiple_of(i * 16, 16), 16)
            scr[a, r, :] = (raw[a, r, :].astype(jnp.float32) * scr_row[...]).astype(jnp.bfloat16)
        each(rows // 16, part)

    kc = min(depth, 1024)
    vb, w = acc.shape[1], acc.shape[2]

    def owned_c(a, b):
        return flip(core, a % 2) + 2 * flip(y, b % 2) + 4 * flip(zl, a // 2) + 8 * flip(zh, b // 2)

    def group(lo, hi, b):
        def mm(a):
            t = a * SIDE + b
            acc[t] = jnp.zeros((vb, w, cols), jnp.float32)

            def kk(k):
                ks = pl.ds(pl.multiple_of(k * kc, kc), kc)
                prod = lax.dot_general(
                    scr[a, :, ks], bb[b, :, ks], (((1,), (1,)), ((), ())),
                    preferred_element_type=jnp.float32,
                )
                acc[t] += prod.reshape(vb, w, cols)
            each(depth // kc, kk)
            other = pl.ds(pl.multiple_of((1 - x) * half, half), half)
            xs[t] = acc[t, :, other, :].astype(jnp.bfloat16)
            xcopy(t).start()
        each(hi, mm, lo)

    def drain(lo, hi, b):
        def fin(a):
            t = a * SIDE + b
            xcopy(t).wait_recv()
            mine = pl.ds(pl.multiple_of(x * half, half), half)
            total = acc[t, :, mine, :] + xr[t].astype(jnp.float32)

            @pl.when(a == 0)
            def _():
                out[:, pl.ds(owned_c(0, b), 1), :, :] = total[:, None]

            @pl.when(a > 0)
            def _():
                zs[t] = total.astype(jnp.bfloat16)
                zcopy(t).start()
        each(hi, fin, lo)

    own_a.wait()
    screen(0)
    own_b.wait()
    a1.wait_recv()
    screen(1)
    group(0, 2, 0)

    def pass_a(k):
        a2(k).wait_recv()
        a3(k).start()

    def pass_b(k):
        b2(k).wait_recv()
        b3(k).start()

    def take_a():
        each(CHUNKS, lambda k: a3(k).wait_recv())
        screen(2)
        screen(3)

    @pl.when(end)
    def _():
        each(CHUNKS, pass_b)
        drain(0, 2, 0)
        b1.wait_recv()
        each(3, lambda b: group(0, 2, b), 1)
        each(3, lambda b: drain(0, 2, b), 1)
        each(CHUNKS, pass_a)
        take_a()
        each(3, lambda b: group(2, 4, b))
        each(3, lambda b: drain(2, 4, b))

    @pl.when(jnp.logical_not(end))
    def _():
        each(CHUNKS, pass_a)
        each(CHUNKS, lambda k: b2(k).wait_send())
        each(CHUNKS, lambda k: a2(k).start())
        drain(0, 2, 0)
        take_a()
        group(2, 4, 0)
        b1.wait_recv()
        group(0, 4, 1)
        drain(2, 4, 0)
        drain(0, 4, 1)
        each(CHUNKS, pass_b)
        group(0, 4, 2)
        drain(0, 4, 2)

    each(CHUNKS, lambda k: b3(k).wait_recv())
    group(0, 4, 3)
    drain(0, 4, 3)

    def land(t):
        zcopy(t).wait_recv()
        c = owned_c(t // SIDE, t % SIDE)
        out[:, pl.ds(c, 1), :, :] = zr[t].astype(jnp.float32)[:, None]
    each(SIDE * SIDE, land, SIDE)

    a1.wait_send()
    b1.wait_send()

    def sent(k):
        a2(k).wait_send()
        a3(k).wait_send()
        b3(k).wait_send()
    each(CHUNKS, sent)

    @pl.when(end)
    def _():
        each(CHUNKS, lambda k: b2(k).wait_send())
    each(SIDE * SIDE, lambda t: xcopy(t).wait_send())
    each(SIDE * SIDE, lambda t: zcopy(t).wait_send(), SIDE)


def grid_body(valence_pairs, conduction_pairs, screening):
    vb, w, depth = valence_pairs.shape
    bands, conduction, _ = conduction_pairs.shape
    cols = bands * conduction
    rows = vb * w
    half = w // lax.axis_size("pw")
    total_c = bands * lax.axis_size("pair")
    tiles = SIDE * SIDE
    dma = pltpu.SemaphoreType.DMA
    bf16 = jnp.bfloat16
    return pl.pallas_call(
        grid_kernel,
        out_shape=jax.ShapeDtypeStruct((vb, total_c, half, conduction), jnp.float32),
        in_specs=[
            pl.BlockSpec(memory_space=pl.ANY),
            pl.BlockSpec(memory_space=pl.ANY),
            pl.BlockSpec(memory_space=pltpu.VMEM),
        ],
        out_specs=pl.BlockSpec(memory_space=pltpu.VMEM),
        scratch_shapes=[
            pltpu.VMEM((SIDE, rows, depth), bf16),
            pltpu.VMEM((SIDE, rows, depth), bf16),
            pltpu.VMEM((SIDE, cols, depth), bf16),
            pltpu.VMEM((tiles, vb, w, cols), jnp.float32),
            pltpu.VMEM((tiles, vb, half, cols), bf16),
            pltpu.VMEM((tiles, vb, half, cols), bf16),
            pltpu.VMEM((tiles, vb, half, cols), bf16),
            pltpu.VMEM((tiles, vb, half, cols), bf16),
            dma((2,)),
            dma((1,)), dma((1,)),
            dma((CHUNKS,)), dma((CHUNKS,)), dma((CHUNKS,)), dma((CHUNKS,)),
            dma((1,)), dma((1,)),
            dma((CHUNKS,)), dma((CHUNKS,)), dma((CHUNKS,)), dma((CHUNKS,)),
            dma((tiles,)), dma((tiles,)), dma((tiles,)), dma((tiles,)),
        ],
        compiler_params=pltpu.CompilerParams(
            collective_id=0, has_side_effects=True, vmem_limit_bytes=56 * 1024 * 1024
        ),
    )(
        valence_pairs.reshape(rows, depth),
        conduction_pairs.reshape(cols, depth),
        screening.reshape(1, depth),
    )


def solution(mesh):
    placed = (P("pair", None, "pw"), P("pair", None, "pw"), P("pw"))
    squared = mesh.shape["pw"] == 2 and mesh.shape["pair"] == SIDE * SIDE

    def body(valence_pairs, conduction_pairs, screening):
        if squared and conduction_pairs.shape[0] == 1:
            return grid_body(valence_pairs, conduction_pairs, screening)
        return general_body(valence_pairs, conduction_pairs, screening)

    return jax.shard_map(
        body, mesh=mesh, in_specs=placed, out_specs=P("pair", None, "pw", None), check_vma=False
    )
```

time: 314 us -> 138 us (0.44)
  waiting for transfers between devices: 224 us -> 0 us
  Pallas kernels: 0 us -> 134 us
  blocking collectives: 53.1 us -> 0 us
  matrix products: 17.2 us -> 0 us
  between operations: 13.4 us -> 0.01 us
  other arithmetic: 3.53 us -> 0 us
    all_gather x1 -> x0, waiting for transfers between devices: 169 us -> none  [body(): lax.all_gather(screened, 'pair', axis=0, tiled=True)]
    pallas_call x0 -> x1, Pallas kernels: none -> 134 us  [grid_body(): pl.pallas_call(grid_kernel, out_shape=jax.ShapeDtypeStruct((vb, total_c,...]
    reduce_scatter x1 -> x0, waiting for transfers between devices: 54.9 us -> none  [body(): lax.psum_scatter(partial_value, 'pw', scatter_dimension=1, tiled=True)]
    all_to_all x1 -> x0, blocking collectives: 53.1 us -> none  [route_rows(): lax.all_to_all(terms, 'pair', split_axis=0, concat_axis=2, tiled=True)]
    dot_general x1 -> x0, matrix products: 17.2 us -> none  [contract(): lax.dot_general(piece.reshape(first * second, width), flat_right, (((1,),...]
    convert_element_type x1 -> x0, other arithmetic: 3.53 us -> none  [body(): (valence_pairs.astype(jnp.float32) * screening[None, None, :]).astype(jnp...]
    unnamed x2 -> x1, local copies, waits for them, and re-layouts: 0.01 us -> 3.16 us
  transfers between devices with their start and end apart: 2 -> 0, of which waited for: 2 -> 0; matrix products, arithmetic and copies ran while one was open for 0% -> 0% of each run, Pallas kernels for 0% -> 0%
where the time goes in v1:
time: 138 us; the launch traced here: 137 us
  Pallas kernels  134 us (97%)
  local copies, waits for them, and re-layouts  3.16 us (2%)
    pallas_call x1, Pallas kernels, grid_body(): pl.pallas_call(grid_kernel, out_shape=jax.ShapeDtypeStruct((vb, total_c,...  134 us
    unnamed x1, local copies, waits for them, and re-layouts  3.16 us

profile of v1, /device:TPU:12, one launch (start us, length us, event | category | flops | bytes accessed | tf_op | source)
XLA Modules:
  0.0 137.4 jit_solution(8171705547751794271)
XLA Ops:
  0.0 134.3 %shard_map.37 = f32[4,16,32,256]{3,2,1,0:T(8,128)} custom-call(bf16[256,4096]{1,0:T(8,128)(2,1)} %bitcast.3, bf16[256,4096]{1,0:T(8,128)(2,1)} %bitcast.4, f32[1,4096]{1,0:T(1,128)} %bitcast.5), custom_call_target="tpu_custom_call" | custom-call | tf_op jit(solution)/shard_map/pallas_call | solution.py:252
  134.3 3.2 %copy.5 = f32[4,16,32,256]{3,2,1,0:T(8,128)} copy(f32[4,16,32,256]{3,2,1,0:T(8,128)} %shard_map.37) | data formatting | bytes 4194304

commit v2 on v1

--- a/solution.py
+++ b/solution.py
@@ -9,7 +9,7 @@
 
 MESH = pl.DeviceIdType.MESH
 SIDE = 4
-CHUNKS = 4
+CHUNKS = 16
 
 
 def contract(piece, flat_right, band_dev, conduction):
@@ -124,7 +124,6 @@
             scr[a, r, :] = (raw[a, r, :].astype(jnp.float32) * scr_row[...]).astype(jnp.bfloat16)
         each(rows // 16, part)
 
-    kc = min(depth, 1024)
     vb, w = acc.shape[1], acc.shape[2]
 
     def owned_c(a, b):
@@ -133,16 +132,10 @@
     def group(lo, hi, b):
         def mm(a):
             t = a * SIDE + b
-            acc[t] = jnp.zeros((vb, w, cols), jnp.float32)
-
-            def kk(k):
-                ks = pl.ds(pl.multiple_of(k * kc, kc), kc)
-                prod = lax.dot_general(
-                    scr[a, :, ks], bb[b, :, ks], (((1,), (1,)), ((), ())),
-                    preferred_element_type=jnp.float32,
-                )
-                acc[t] += prod.reshape(vb, w, cols)
-            each(depth // kc, kk)
+            prod = lax.dot_general(
+                scr[a], bb[b], (((1,), (1,)), ((), ())), preferred_element_type=jnp.float32
+            )
+            acc[t] = prod.reshape(vb, w, cols)
             other = pl.ds(pl.multiple_of((1 - x) * half, half), half)
             xs[t] = acc[t, :, other, :].astype(jnp.bfloat16)
             xcopy(t).start()

time: 138 us -> 133 us (0.964)
  Pallas kernels: 134 us -> 130 us
    pallas_call x1, Pallas kernels: 134 us -> 130 us  [grid_body(): pl.pallas_call(grid_kernel, out_shape=jax.ShapeDtypeStruct((vb, total_c,...]
where the time goes in v2:
time: 133 us
  Pallas kernels  130 us (98%)
  local copies, waits for them, and re-layouts  3.16 us (2%)
    pallas_call x1, Pallas kernels, grid_body(): pl.pallas_call(grid_kernel, out_shape=jax.ShapeDtypeStruct((vb, total_c,...  130 us
    unnamed x1, local copies, waits for them, and re-layouts  3.16 us

profile of v2, /device:TPU:12, one launch (start us, length us, event | category | flops | bytes accessed | tf_op | source)
XLA Modules:
  0.0 132.9 jit_solution(17207500766257402981)
XLA Ops:
  0.0 129.7 %shard_map.37 = f32[4,16,32,256]{3,2,1,0:T(8,128)} custom-call(bf16[256,4096]{1,0:T(8,128)(2,1)} %bitcast.3, bf16[256,4096]{1,0:T(8,128)(2,1)} %bitcast.4, f32[1,4096]{1,0:T(1,128)} %bitcast.5), custom_call_target="tpu_custom_call" | custom-call | tf_op jit(solution)/shard_map/pallas_call | solution.py:245
  129.7 3.2 %copy.5 = f32[4,16,32,256]{3,2,1,0:T(8,128)} copy(f32[4,16,32,256]{3,2,1,0:T(8,128)} %shard_map.37) | data formatting | bytes 4194304
